TPU v7x, 32 devices: a whole 2x2x4 slice. The times are simulated.
32 devices in a mesh: patch: 16 (over z, y, x), sub: 2 (over core).
Axes of the slice: x: 2, y: 2, z: 4, core: 2. Of those that a mesh axis runs over, the one named last changes fastest.
Arguments:
- fields: float32 [5, 64, 128, 128], P(None, ('patch', 'sub')), may hold values from -6 to 6
- density: float32 [64, 128, 128], P(('patch', 'sub')), may hold values from 1 to 3
- moduli: float32 [2, 64, 128, 128], P(None, ('patch', 'sub')), may hold values from 0.5 to 128
- metric_diag: float32 [2, 64, 128, 128], P(None, ('patch', 'sub')), may hold values from 0.7 to 1.3
- metric_cross: float32 [2, 64, 128, 128], P(None, ('patch', 'sub')), may hold values from -0.3 to 0.3
- fc_extension: float32 [25, 10], replicated, may hold values from -2 to 2
- patch_count: int32 [32], P(('patch', 'sub')), may hold values from 1 to 2, as said below
- connectivity: int32 [256, 3], P(('patch', 'sub')), may hold values from -1 to 31, as said below
Outputs:
- advanced: float32 [5, 64, 128, 128], P(None, ('patch', 'sub'))
Inputs may be any that keep to these rules, and one draw needn't show every extreme that they name: `patch_count`: every device holds at most 2 live patches; the largest count is 2 in every draw. `connectivity`: links join only live slots and are symmetric with equal orientation flags on both ends; a neighbour is held by the same device or by the device whose flat index differs by 1 or 17 modulo 32; from one device to another device go at most 2 linked sides, and this number is reached in every draw.
All inputs are finite; a program needn't handle non-finite values.
Results may differ from a plain program's by a relative error of at most 0.00005.
Values sent between devices are 32-bit elements; how exact they have to be, the bound alone decides.
A program may use at most 64 MiB of HBM per device.

v0:
```python
import functools

import jax
import jax.numpy as jnp
import numpy as np
from jax import lax
from jax.experimental import pallas as pl
from jax.experimental.pallas import tpu as pltpu
from jax.sharding import PartitionSpec as P

MESH = pl.DeviceIdType.MESH
ROWS = 8
cfl_number = 0.5
penalty_weight = 0.5


def circulant(points, extra):
    length = points + extra
    half = (length - 1) // 2
    waves = np.arange(1, half + 1, dtype=np.float64)
    weights = waves * (2.0 * np.pi * (points - 1) / length)
    shifts = np.arange(length)
    phase = 2.0 * np.pi / length * (waves[:, None] * shifts[None, :] % length)
    kernel = -(2.0 / length) * np.sum(weights[:, None] * np.sin(phase), axis=0)
    at = (np.arange(points)[:, None] - np.arange(length)[None, :]) % length
    full = kernel[at].astype(np.float32)
    padded = -(-extra // ROWS) * ROWS
    outer = np.zeros((points, points), np.float32)
    outer[:, :extra] = full[:, points:]
    return full[:, :points], outer, padded


def split(x):
    hi = x.astype(jnp.bfloat16)
    lo = (x - hi.astype(jnp.float32)).astype(jnp.bfloat16)
    return hi, lo


def kernel(
    total, subs, offsets, reach,
    conn_hbm, count_hbm, fields_hbm, density_hbm, moduli_hbm, diag_hbm, cross_hbm,
    ext_hbm, inner_hbm, outer_hbm,
    out_v,
    conn, count, ext, inner, outer,
    fld, den, mod, dia, cro, rate1, dxi, deta, left, right, ext_v, cols, trans,
    lines, lines2, turned1, turned2, outbox1, outbox2, inbox1, inbox2, corner, corners,
    mine, gather,
    load_sem, send1, recv1, send2, recv2, csend, crecv, bsend, brecv,
):
    comps, slots, n, _ = fld.shape
    sides = slots * 4
    chunks = n // ROWS
    me = lax.axis_index("patch") * subs + lax.axis_index("sub")

    def place(flat):
        return (lax.div(flat, subs), lax.rem(flat, subs))

    def away(off):
        return lax.rem(me + off, total)

    loads = []
    for at, (src, dst) in enumerate(
        (
            (conn_hbm, conn), (count_hbm, count), (ext_hbm, ext), (inner_hbm, inner),
            (outer_hbm, outer), (fields_hbm, fld), (density_hbm, den), (moduli_hbm, mod),
            (diag_hbm, dia), (cross_hbm, cro),
        )
    ):
        if src is fields_hbm:
            for f in range(comps):
                pltpu.make_async_copy(src.at[f], dst.at[f], load_sem.at[at]).start()
        else:
            pltpu.make_async_copy(src, dst, load_sem.at[at]).start()
        loads.append(pltpu.make_async_copy(src, dst, load_sem.at[at]))

    barrier = pltpu.get_barrier_semaphore()

    def greet(d, _):
        pl.semaphore_signal(barrier, inc=1, device_id=place(away(d)), device_id_type=MESH)
        return _

    lax.fori_loop(1, total, greet, 0)

    lines[...] = jnp.zeros_like(lines)
    lines2[...] = jnp.zeros_like(lines2)
    trans[...] = jnp.zeros_like(trans)
    ext_v[...] = jnp.zeros_like(ext_v)

    loads[0].wait()
    loads[1].wait()
    near = [away(off) for off in offsets]
    owner = [conn[0, s] for s in range(sides)]
    linked = [owner[s] >= 0 for s in range(sides)]
    strip = [jnp.where(linked[s], conn[1, s], 0) for s in range(sides)]
    flip = [conn[2, s] for s in range(sides)]
    picks = []
    for peer in near:
        seen = jnp.int32(0)
        pick = [jnp.int32(0)] * slots
        for s in range(sides):
            hit = owner[s] == peer
            for k in range(slots):
                pick[k] = jnp.where(hit & (seen == k), s, pick[k])
            seen = seen + hit.astype(jnp.int32)
        picks.append(pick)
    box, local = [], []
    for s in range(sides):
        pos = jnp.int32(0)
        for t in range(sides):
            if t != s:
                pos = pos + ((owner[t] == owner[s]) & (strip[t] < strip[s])).astype(jnp.int32)
        pos = jnp.minimum(pos, slots - 1)
        at = pos
        for o, off in enumerate(offsets):
            at = jnp.where(owner[s] == away(total - off), o * slots + pos, at)
        box.append(at)
        local.append(owner[s] == me)

    lane = lax.broadcasted_iota(jnp.int32, (ROWS, n), 1)
    row = lax.broadcasted_iota(jnp.int32, (ROWS, n), 0)
    low, high = lane == 0, lane == n - 1
    edge = low | high
    used = row < comps
    pairs = [(f, p, p * 8 + f) for p in range(slots) for f in range(comps)]
    weight = penalty_weight * (n - 1)

    def collect(state, lines):
        def columns(c, _):
            rows = pl.ds(pl.multiple_of(c * ROWS, ROWS), ROWS)
            acc = jnp.zeros((ROWS, n), jnp.float32)
            for f, p, m in pairs:
                turned = pltpu.roll(state[f, p, rows, :], 2 * m + 1, 1)
                acc = jnp.where((lane == 2 * m) | (lane == 2 * m + 1), turned, acc)
            cols[rows, :] = acc
            return _

        lax.fori_loop(0, chunks, columns, 0, unroll=chunks)
        trans[...] = jnp.transpose(cols[...])
        for p in range(slots):
            lines[p * 4 + 2] = trans[pl.ds(p * 16 + 1, 8, stride=2), :]
            lines[p * 4 + 3] = trans[pl.ds(p * 16, 8, stride=2), :]
            for f in range(comps):
                lines[p * 4, pl.ds(f, 1)] = state[f, p, pl.ds(0, 1), :]
                lines[p * 4 + 1, pl.ds(f, 1)] = state[f, p, pl.ds(n - 1, 1), :]

    def turn(lines, turned):
        for s in range(sides):
            index = jnp.where(flip[s] == 1, n - 1 - lane, lane)
            turned[s] = jnp.take_along_axis(lines[s], index, axis=1)

    def post(turned, outbox, inbox, send, recv):
        for o in range(len(offsets)):
            for k in range(slots):
                outbox[o, k] = turned[picks[o][k]]
        sent = []
        for o in range(len(offsets)):
            copy = pltpu.make_async_remote_copy(
                src_ref=outbox.at[o, :, pl.ds(0, comps), :],
                dst_ref=inbox.at[pl.ds(o * slots, slots), pl.ds(0, comps), :],
                send_sem=send.at[o],
                recv_sem=recv.at[o],
                device_id=place(near[o]),
                device_id_type=MESH,
            )
            copy.start()
            sent.append(copy)
        return sent

    def partners(turned, inbox):
        return [
            jnp.where(used, jnp.where(local[s], turned[strip[s]], inbox[box[s]]), 0.0)
            for s in range(sides)
        ]

    def spread(jump):
        for p in range(slots):
            trans[pl.ds(p * 16 + 1, 8, stride=2), :] = jump[p * 4 + 2]
            trans[pl.ds(p * 16, 8, stride=2), :] = jump[p * 4 + 3]
        cols[...] = jnp.transpose(trans[...])

    def derive(state):
        for f in range(comps):
            h0, l0 = split(state[f, 0])
            h1, l1 = split(state[f, 1])
            rows = jnp.concatenate(
                [jnp.concatenate([h0, l0], axis=1), jnp.concatenate([h1, l1], axis=1)], axis=0
            )
            eta = jnp.dot(rows, right[...], preferred_element_type=jnp.float32)
            both = eta[:, :n] + eta[:, n:]
            deta[f, 0] = both[:n]
            deta[f, 1] = both[n:]
            body = jnp.concatenate(
                [jnp.concatenate([h0, h1], axis=1), jnp.concatenate([l0, l1], axis=1)], axis=0
            )
            xi = jnp.dot(left[...], body, preferred_element_type=jnp.float32)
            both = xi[:n] + xi[n:]
            dxi[f, 0] = both[:, :n]
            dxi[f, 1] = both[:, n:]

    def interior(keep):
        for p in range(slots):

            def body(c, _):
                rows = pl.ds(pl.multiple_of(c * ROWS, ROWS), ROWS)
                xx, yy = dia[0, p, rows, :], dia[1, p, rows, :]
                xy, ex = cro[0, p, rows, :], cro[1, p, rows, :]
                lame, shear = mod[0, p, rows, :], mod[1, p, rows, :]
                inv = den[p, rows, :]
                stiff = lame + 2.0 * shear
                ax = [dxi[f, p, rows, :] for f in range(comps)]
                ay = [deta[f, p, rows, :] for f in range(comps)]
                gx = [xx * a + ex * b for a, b in zip(ax, ay)]
                gy = [xy * a + yy * b for a, b in zip(ax, ay)]
                keep(0, p, rows, (gx[2] + gy[4]) * inv)
                keep(1, p, rows, (gx[4] + gy[3]) * inv)
                keep(2, p, rows, stiff * gx[0] + lame * gy[1])
                keep(3, p, rows, lame * gx[0] + stiff * gy[1])
                keep(4, p, rows, shear * (gy[0] + gx[1]))
                return _

            lax.fori_loop(0, chunks, body, 0, unroll=chunks)

    def add_rows(state, jump):
        for p in range(slots):
            for f in range(comps):
                for side, at in ((0, 0), (1, n - 1)):
                    spot = pl.ds(at, 1)
                    state[f, p, spot, :] = state[f, p, spot, :] + jump[p * 4 + side][f : f + 1]

    def add_columns(state):
        def body(c, _):
            rows = pl.ds(pl.multiple_of(c * ROWS, ROWS), ROWS)
            both = cols[rows, :]
            for f, p, m in pairs:
                side = pltpu.roll(both, n - (2 * m + 1), 1)
                state[f, p, rows, :] = state[f, p, rows, :] + jnp.where(edge, side, 0.0)
            return _

        lax.fori_loop(0, chunks, body, 0, unroll=chunks)

    for at in (2, 3, 4):
        loads[at].wait()
    twice, extra = ext.shape
    ext_v[pl.ds(0, twice), pl.ds(0, extra)] = ext[...]
    turned = pltpu.roll(ext_v[...], n - twice // 2, 0)
    matrix = inner[...] + lax.dot_general(
        outer[...],
        turned,
        (((1,), (1,)), ((), ())),
        precision=lax.Precision.HIGHEST,
        preferred_element_type=jnp.float32,
    )
    hi, lo = split(matrix)
    none = jnp.zeros_like(hi)
    left[...] = jnp.concatenate(
        [jnp.concatenate([hi, hi], axis=1), jnp.concatenate([lo, none], axis=1)], axis=0
    )
    hi, lo = split(jnp.transpose(matrix))
    right[...] = jnp.concatenate(
        [jnp.concatenate([hi, lo], axis=1), jnp.concatenate([hi, none], axis=1)], axis=0
    )

    loads[5].wait()
    collect(fld, lines)
    turn(lines, turned1)
    tile = jnp.zeros((ROWS, n), jnp.float32)
    for p in range(slots):
        for b in range(2):
            first = p * 4 + 2 * b
            rolled = pltpu.roll(lines[p * 4 + b], first + 1, 1)
            tile = jnp.where((lane == first) | (lane == first + 1), rolled, tile)
    for r in range(3):
        for s in range(sides):
            tile = jnp.where(
                (row == comps + r) & (lane == s), conn[r, s].astype(jnp.float32), tile
            )
    packed = jnp.sum(
        pltpu.roll(tile, 0, 1, stride=sides, stride_axis=0), axis=0, keepdims=True
    )
    corner[...] = packed
    corners[0] = packed

    pl.semaphore_wait(barrier, total - 1)
    sent1 = post(turned1, outbox1, inbox1, send1, recv1)
    sentc = []
    for j, off in enumerate(reach):
        if j > 0:
            there = reach.index(total - off)
            copy = pltpu.make_async_remote_copy(
                src_ref=corner,
                dst_ref=corners.at[there],
                send_sem=csend.at[j - 1],
                recv_sem=crecv.at[there - 1],
                device_id=place(away(off)),
                device_id_type=MESH,
            )
            copy.start()
            sentc.append(copy)

    for load in loads[6:]:
        load.wait()
    top = jnp.zeros((ROWS, n), jnp.float32)
    for p in range(slots):

        def speeds(c, top):
            rows = pl.ds(pl.multiple_of(c * ROWS, ROWS), ROWS)
            xx, yy = dia[0, p, rows, :], dia[1, p, rows, :]
            xy, ex = cro[0, p, rows, :], cro[1, p, rows, :]
            stiff = mod[0, p, rows, :] + 2.0 * mod[1, p, rows, :]
            inv = 1.0 / den[p, rows, :]
            den[p, rows, :] = inv
            speed = jnp.sqrt(stiff * inv) * (
                jnp.sqrt(xx * xx + xy * xy) + jnp.sqrt(ex * ex + yy * yy)
            )
            return jnp.maximum(top, speed)

        part = lax.fori_loop(
            0, chunks, speeds, jnp.zeros((ROWS, n), jnp.float32), unroll=chunks
        )
        top = jnp.maximum(top, jnp.where(count[0] > p, part, 0.0))
    mine[...] = jnp.max(top, axis=0, keepdims=True)

    def tell(d, _):
        pltpu.make_async_remote_copy(
            src_ref=mine,
            dst_ref=gather.at[d - 1],
            send_sem=bsend.at[0],
            recv_sem=brecv.at[0],
            device_id=place(away(d)),
            device_id_type=MESH,
        ).start()
        return _

    lax.fori_loop(1, total, tell, 0)

    derive(fld)

    def keep1(f, p, rows, value):
        rate1[f, p, rows, :] = value

    interior(keep1)
    collect(rate1, lines2)
    turn(lines2, turned2)
    sent2 = post(turned2, outbox2, inbox2, send2, recv2)

    for copy in sent1 + sentc:
        copy.wait_recv()
    other = partners(turned1, inbox1)
    jump1 = [jnp.where(linked[s], weight * (other[s] - lines[s]), 0.0) for s in range(sides)]
    spread(jump1)
    add_rows(rate1, jump1)
    add_columns(rate1)

    def whole(value):
        return jnp.broadcast_to(value, (ROWS, n))

    table = jnp.zeros((ROWS, n), jnp.float32)
    for j in range(len(reach)):
        index = (lane - j * sides + row * sides) & (n - 1)
        laid = jnp.take_along_axis(whole(corners[j]), index, axis=1)
        table = jnp.where((lane >= j * sides) & (lane < (j + 1) * sides), laid, table)
    their_owner = jnp.full((ROWS, n), -1, jnp.int32)
    their_strip = jnp.zeros((ROWS, n), jnp.int32)
    their_flip = jnp.zeros((ROWS, n), jnp.int32)
    for s in range(sides):
        here = lax.shift_right_logical(lane, 1) == s
        their_owner = jnp.where(here, owner[s], their_owner)
        their_strip = jnp.where(here, strip[s], their_strip)
        their_flip = jnp.where(here, flip[s], their_flip)

    def seat(device):
        at = jnp.zeros((ROWS, n), jnp.int32)
        for j, off in enumerate(reach):
            at = jnp.where(device == away(off), j * sides, at)
        return at

    def nook(strip, end):
        b = strip & 1
        across = (strip & 2) == 0
        return (strip & ~3) + jnp.where(across, 2 * b + 1 - end, 2 * end + 1 - b)

    end = (1 - (lane & 1)) ^ (their_flip & 1)
    base = seat(their_owner)
    beside = (their_strip & ~3) + jnp.where((their_strip & 2) == 0, 2 + end, end)
    entry = jnp.take_along_axis(table, base + beside, axis=1)
    own = jnp.take_along_axis(table, base + nook(their_strip, end), axis=1)
    far_owner = whole(entry[comps : comps + 1]).astype(jnp.int32)
    far_strip = whole(entry[comps + 1 : comps + 2]).astype(jnp.int32)
    far_flip = whole(entry[comps + 2 : comps + 3]).astype(jnp.int32)
    far_strip = jnp.where(far_owner >= 0, far_strip, 0)
    far_end = (their_strip & 1) ^ (far_flip & 1)
    value = jnp.take_along_axis(table, seat(far_owner) + nook(far_strip, far_end), axis=1)
    bend = jnp.where((far_owner >= 0) & used, weight * (value - own), 0.0)

    rest = []
    for p in range(slots):
        west, east, south, north = jump1[p * 4 : p * 4 + 4]
        mixed = (
            jnp.where(low, south, 0.0) + jnp.where(high, pltpu.roll(north, n - 1, 1), 0.0),
            jnp.where(low, pltpu.roll(south, 1, 1), 0.0) + jnp.where(high, north, 0.0),
            jnp.where(low, west, 0.0) + jnp.where(high, pltpu.roll(east, n - 1, 1), 0.0),
            jnp.where(low, pltpu.roll(west, 1, 1), 0.0) + jnp.where(high, east, 0.0),
        )
        for side in range(4):
            s = p * 4 + side
            theirs = jnp.where(edge, pltpu.roll(bend, n - (2 * s + 1), 1), 0.0)
            rest.append(theirs - mixed[side] - 2.0 * jump1[s] - lines2[s])

    derive(rate1)

    pltpu.make_async_copy(gather, gather, brecv.at[0]).wait()
    best = mine[...]
    for d in range(total - 1):
        best = jnp.maximum(best, gather[d])
    bound = jnp.max(best, axis=1, keepdims=True)
    step = jnp.broadcast_to(cfl_number / (bound * (n - 1)), (ROWS, n))
    half = 0.5 * step * step

    def keep2(f, p, rows, second):
        value = fld[f, p, rows, :] + step * rate1[f, p, rows, :] + half * second
        out_v[f, p, rows, :] = jnp.where(count[0] > p, value, 0.0)

    interior(keep2)

    for copy in sent2:
        copy.wait_recv()
    other = partners(turned2, inbox2)
    jump2 = [
        jnp.where(linked[s], (half * weight) * (other[s] + rest[s]), 0.0) for s in range(sides)
    ]
    spread(jump2)
    add_rows(out_v, jump2)
    add_columns(out_v)

    for copy in sent1 + sentc + sent2:
        copy.wait_send()
    pltpu.make_async_copy(gather, gather, bsend.at[0]).wait()


def shards(
    total, subs, fields, density, moduli, metric_diag, metric_cross, extension, count, connectivity
):
    comps, slots, n, _ = fields.shape
    inner, outer, _ = circulant(n, extension.shape[0])
    far = total // 2 + 1
    offsets = (1, total - 1, far, total - far)
    reach = [0, *offsets]
    for a in offsets:
        for b in offsets:
            if (a + b) % total not in reach:
                reach.append((a + b) % total)
    f32, i32 = jnp.float32, jnp.int32
    hbm = pl.BlockSpec(memory_space=pltpu.HBM)
    state = pltpu.VMEM(fields.shape, f32)
    square = pltpu.VMEM((n, n), f32)
    dma = pltpu.SemaphoreType.DMA
    boxed = pltpu.VMEM((4, slots, 8, n), f32)
    arrived = pltpu.VMEM((4 * slots, 8, n), f32)
    strips = pltpu.VMEM((slots * 4, 8, n), f32)
    return pl.pallas_call(
        functools.partial(kernel, total, subs, offsets, reach),
        out_shape=pltpu.VMEM(fields.shape, f32),
        in_specs=[hbm] * 10,
        out_specs=pl.BlockSpec(memory_space=pltpu.VMEM),
        scratch_shapes=[
            pltpu.SMEM(connectivity.shape[::-1], i32),
            pltpu.SMEM(count.shape, i32),
            pltpu.VMEM(extension.shape[::-1], f32),
            square, square,
            state,
            pltpu.VMEM(density.shape, f32),
            pltpu.VMEM(moduli.shape, f32),
            pltpu.VMEM(metric_diag.shape, f32),
            pltpu.VMEM(metric_cross.shape, f32),
            state, state, state,
            pltpu.VMEM((2 * n, 2 * n), jnp.bfloat16),
            pltpu.VMEM((2 * n, 2 * n), jnp.bfloat16),
            square, square, square,
            strips, strips, strips, strips,
            boxed, boxed, arrived, arrived,
            pltpu.VMEM((1, n), f32),
            pltpu.VMEM((len(reach), 1, n), f32),
            pltpu.VMEM((1, n), f32),
            pltpu.VMEM((total - 1, 1, n), f32),
            dma((10,)),
            dma((4,)), dma((4,)), dma((4,)), dma((4,)),
            dma((len(reach) - 1,)), dma((len(reach) - 1,)), dma((1,)), dma((1,)),
        ],
        compiler_params=pltpu.CompilerParams(collective_id=0, has_side_effects=True),
    )(connectivity.T, count, fields, density, moduli, metric_diag, metric_cross, extension.T,
      jnp.asarray(inner), jnp.asarray(outer))


def solution(mesh):
    placed = (
        P(None, ("patch", "sub"), None, None),
        P(("patch", "sub"), None, None),
        P(None, ("patch", "sub"), None, None),
        P(None, ("patch", "sub"), None, None),
        P(None, ("patch", "sub"), None, None),
        P(),
        P(("patch", "sub")),
        P(("patch", "sub"), None),
    )
    total = mesh.shape["patch"] * mesh.shape["sub"]
    return jax.shard_map(
        functools.partial(shards, total, mesh.shape["sub"]),
        mesh=mesh,
        in_specs=placed,
        out_specs=P(None, ("patch", "sub"), None, None),
        check_vma=False,
    )
```

profile of v0, /device:TPU:0, one launch (start us, length us, event | category | flops | bytes accessed | tf_op | source)
XLA Modules:
  0.0 13.7 jit_solution(13618024139379054728)
XLA Ops:
  0.7 12.2 %shard_map.100 = f32[5,2,128,128]{3,2,1,0:T(8,128)S(1)} custom-call(s32[3,8]{1,0:T(4,128)} %bitcast.3, s32[1]{0:T(128)S(6)} %copy.13.count_hbm, f32[5,2,128,128]{3,2,1,0:T(8,128)} %fields_hbm.1, f32[2,128,128]{2,1,0:T(8,128)} %density_hbm.1, f32[2,2,128,128]{3,2,1,0:T(8,128)} %moduli_hbm.1, f32[2,2,128,128]{3,2,1,0:T(8,128)} %diag_hbm.1, ...), custom_call_target="tpu_custom_call" | custom-call | tf_op jit(solution)/shard_map/pallas_call | solution.py:460
  12.9 0.8 %copy.12 = f32[5,2,128,128]{3,2,1,0:T(8,128)} copy(f32[5,2,128,128]{3,2,1,0:T(8,128)S(1)} %shard_map.100) | data formatting | bytes 1310720
where the time goes:
time: 13.9 us; the launch traced here: 13.7 us
  Pallas kernels  12.2 us (88%)
  local copies, waits for them, and re-layouts  0.84 us (6%)
  between operations  0.66 us (5%)
    pallas_call x1, Pallas kernels, shards(): pl.pallas_call(functools.partial(kernel, total, subs, offsets, reach), ou...  12.2 us
    unnamed x1, local copies, waits for them, and re-layouts  0.84 us

commit v1 on v0

--- a/solution.py
+++ b/solution.py
@@ -39,82 +39,87 @@
 def kernel(
     total, subs, offsets, reach,
     conn_hbm, count_hbm, fields_hbm, density_hbm, moduli_hbm, diag_hbm, cross_hbm,
-    ext_hbm, inner_hbm, outer_hbm,
+    ext_hbm, consts_hbm,
     out_v,
-    conn, count, ext, inner, outer,
-    fld, den, mod, dia, cro, rate1, dxi, deta, left, right, ext_v, cols, trans,
+    conn, count, ext, consts,
+    fld, med, rate1, dxi, deta, left, right, ext_v, cols, trans,
     lines, lines2, turned1, turned2, outbox1, outbox2, inbox1, inbox2, corner, corners,
     mine, gather,
-    load_sem, send1, recv1, send2, recv2, csend, crecv, bsend, brecv,
+    load_sem, send_sem, recv_sem,
 ):
     comps, slots, n, _ = fld.shape
     sides = slots * 4
     chunks = n // ROWS
-    me = lax.axis_index("patch") * subs + lax.axis_index("sub")
+    patch, core = lax.axis_index("patch"), lax.axis_index("sub")
+    me = patch * subs + core
+    simple = total & (total - 1) == 0 and subs & (subs - 1) == 0
+    unroll = total - 1 if total <= 64 else 1
+
+    def away(off):
+        return lax.rem(me + off, total)
 
     def place(flat):
         return (lax.div(flat, subs), lax.rem(flat, subs))
 
-    def away(off):
-        return lax.rem(me + off, total)
-
-    loads = []
-    for at, (src, dst) in enumerate(
-        (
-            (conn_hbm, conn), (count_hbm, count), (ext_hbm, ext), (inner_hbm, inner),
-            (outer_hbm, outer), (fields_hbm, fld), (density_hbm, den), (moduli_hbm, mod),
-            (diag_hbm, dia), (cross_hbm, cro),
+    def peer(d):
+        if simple:
+            return (patch ^ lax.div(d, subs), core ^ lax.rem(d, subs))
+        return place(away(d))
+
+    conn_load = pltpu.make_async_copy(conn_hbm, conn, load_sem.at[0])
+    count_load = pltpu.make_async_copy(count_hbm, count, load_sem.at[1])
+    ext_load = pltpu.make_async_copy(ext_hbm, ext, load_sem.at[2])
+    consts_load = pltpu.make_async_copy(consts_hbm, consts, load_sem.at[3])
+    fields_load = pltpu.make_async_copy(fields_hbm, fld, load_sem.at[4])
+    med_load = pltpu.make_async_copy(med, med, load_sem.at[5])
+    conn_load.start()
+    for f in range(comps):
+        pltpu.make_async_copy(fields_hbm.at[f], fld.at[f], load_sem.at[4]).start()
+    ext_load.start()
+    consts_load.start()
+    pltpu.make_async_copy(density_hbm, med.at[0], load_sem.at[5]).start()
+    for k in range(2):
+        pltpu.make_async_copy(moduli_hbm.at[k], med.at[1 + k], load_sem.at[5]).start()
+        pltpu.make_async_copy(diag_hbm.at[k], med.at[3 + k], load_sem.at[5]).start()
+        pltpu.make_async_copy(cross_hbm.at[k], med.at[5 + k], load_sem.at[5]).start()
+    count_load.start()
+
+    barrier = pltpu.get_barrier_semaphore()
+
+    def greet(i, _):
+        pl.semaphore_signal(
+            barrier, inc=1, device_id=peer(total - 1 - i), device_id_type=MESH
         )
-    ):
-        if src is fields_hbm:
-            for f in range(comps):
-                pltpu.make_async_copy(src.at[f], dst.at[f], load_sem.at[at]).start()
-        else:
-            pltpu.make_async_copy(src, dst, load_sem.at[at]).start()
-        loads.append(pltpu.make_async_copy(src, dst, load_sem.at[at]))
-
-    barrier = pltpu.get_barrier_semaphore()
-
-    def greet(d, _):
-        pl.semaphore_signal(barrier, inc=1, device_id=place(away(d)), device_id_type=MESH)
         return _
 
-    lax.fori_loop(1, total, greet, 0)
+    lax.fori_loop(0, total - 1, greet, 0, unroll=unroll)
 
     lines[...] = jnp.zeros_like(lines)
     lines2[...] = jnp.zeros_like(lines2)
     trans[...] = jnp.zeros_like(trans)
     ext_v[...] = jnp.zeros_like(ext_v)
 
-    loads[0].wait()
-    loads[1].wait()
+    conn_load.wait()
     near = [away(off) for off in offsets]
     owner = [conn[0, s] for s in range(sides)]
     linked = [owner[s] >= 0 for s in range(sides)]
     strip = [jnp.where(linked[s], conn[1, s], 0) for s in range(sides)]
     flip = [conn[2, s] for s in range(sides)]
+    tags = []
+    for s in range(sides):
+        rank = jnp.int32(0)
+        for t in range(s):
+            rank = rank + (owner[t] == owner[s]).astype(jnp.int32)
+        tags.append(owner[s] * sides + rank)
     picks = []
-    for peer in near:
-        seen = jnp.int32(0)
-        pick = [jnp.int32(0)] * slots
-        for s in range(sides):
-            hit = owner[s] == peer
-            for k in range(slots):
-                pick[k] = jnp.where(hit & (seen == k), s, pick[k])
-            seen = seen + hit.astype(jnp.int32)
+    for there in near:
+        pick = []
+        for k in range(slots):
+            tag, at = there * sides + k, jnp.int32(0)
+            for s in range(1, sides):
+                at = jnp.where(tags[s] == tag, s, at)
+            pick.append(at)
         picks.append(pick)
-    box, local = [], []
-    for s in range(sides):
-        pos = jnp.int32(0)
-        for t in range(sides):
-            if t != s:
-                pos = pos + ((owner[t] == owner[s]) & (strip[t] < strip[s])).astype(jnp.int32)
-        pos = jnp.minimum(pos, slots - 1)
-        at = pos
-        for o, off in enumerate(offsets):
-            at = jnp.where(owner[s] == away(total - off), o * slots + pos, at)
-        box.append(at)
-        local.append(owner[s] == me)
 
     lane = lax.broadcasted_iota(jnp.int32, (ROWS, n), 1)
     row = lax.broadcasted_iota(jnp.int32, (ROWS, n), 0)
@@ -148,23 +153,26 @@
             index = jnp.where(flip[s] == 1, n - 1 - lane, lane)
             turned[s] = jnp.take_along_axis(lines[s], index, axis=1)
 
-    def post(turned, outbox, inbox, send, recv):
+    def post(turned, outbox, inbox, at):
         for o in range(len(offsets)):
             for k in range(slots):
-                outbox[o, k] = turned[picks[o][k]]
-        sent = []
+                outbox[o * slots + k] = turned[picks[o][k]]
         for o in range(len(offsets)):
-            copy = pltpu.make_async_remote_copy(
-                src_ref=outbox.at[o, :, pl.ds(0, comps), :],
-                dst_ref=inbox.at[pl.ds(o * slots, slots), pl.ds(0, comps), :],
-                send_sem=send.at[o],
-                recv_sem=recv.at[o],
+            spot = (pl.ds(o * slots, slots), pl.ds(0, comps), slice(None))
+            pltpu.make_async_remote_copy(
+                src_ref=outbox.at[spot],
+                dst_ref=inbox.at[spot],
+                send_sem=send_sem.at[at],
+                recv_sem=recv_sem.at[at],
                 device_id=place(near[o]),
                 device_id_type=MESH,
-            )
-            copy.start()
-            sent.append(copy)
-        return sent
+            ).start()
+
+    def settle(buffer, sem):
+        pltpu.make_async_copy(buffer, buffer, sem).wait()
+
+    def carried(buffer):
+        return buffer.at[:, pl.ds(0, comps), :]
 
     def partners(turned, inbox):
         return [
@@ -202,10 +210,7 @@
 
             def body(c, _):
                 rows = pl.ds(pl.multiple_of(c * ROWS, ROWS), ROWS)
-                xx, yy = dia[0, p, rows, :], dia[1, p, rows, :]
-                xy, ex = cro[0, p, rows, :], cro[1, p, rows, :]
-                lame, shear = mod[0, p, rows, :], mod[1, p, rows, :]
-                inv = den[p, rows, :]
+                inv, lame, shear, xx, yy, xy, ex = (med[k, p, rows, :] for k in range(7))
                 stiff = lame + 2.0 * shear
                 ax = [dxi[f, p, rows, :] for f in range(comps)]
                 ay = [deta[f, p, rows, :] for f in range(comps)]
@@ -238,13 +243,14 @@
 
         lax.fori_loop(0, chunks, body, 0, unroll=chunks)
 
-    for at in (2, 3, 4):
-        loads[at].wait()
+    ext_load.wait()
+    consts_load.wait()
+    fields_load.wait()
     twice, extra = ext.shape
     ext_v[pl.ds(0, twice), pl.ds(0, extra)] = ext[...]
     turned = pltpu.roll(ext_v[...], n - twice // 2, 0)
-    matrix = inner[...] + lax.dot_general(
-        outer[...],
+    matrix = consts[0] + lax.dot_general(
+        consts[1],
         turned,
         (((1,), (1,)), ((), ())),
         precision=lax.Precision.HIGHEST,
@@ -260,9 +266,14 @@
         [jnp.concatenate([hi, lo], axis=1), jnp.concatenate([hi, none], axis=1)], axis=0
     )
 
-    loads[5].wait()
     collect(fld, lines)
     turn(lines, turned1)
+
+    pl.semaphore_wait(barrier, total - 1)
+    post(turned1, outbox1, inbox1, 0)
+
+    count_load.wait()
+    med_load.wait()
     tile = jnp.zeros((ROWS, n), jnp.float32)
     for p in range(slots):
         for b in range(2):
@@ -280,36 +291,15 @@
     corner[...] = packed
     corners[0] = packed
 
-    pl.semaphore_wait(barrier, total - 1)
-    sent1 = post(turned1, outbox1, inbox1, send1, recv1)
-    sentc = []
-    for j, off in enumerate(reach):
-        if j > 0:
-            there = reach.index(total - off)
-            copy = pltpu.make_async_remote_copy(
-                src_ref=corner,
-                dst_ref=corners.at[there],
-                send_sem=csend.at[j - 1],
-                recv_sem=crecv.at[there - 1],
-                device_id=place(away(off)),
-                device_id_type=MESH,
-            )
-            copy.start()
-            sentc.append(copy)
-
-    for load in loads[6:]:
-        load.wait()
     top = jnp.zeros((ROWS, n), jnp.float32)
     for p in range(slots):
 
         def speeds(c, top):
             rows = pl.ds(pl.multiple_of(c * ROWS, ROWS), ROWS)
-            xx, yy = dia[0, p, rows, :], dia[1, p, rows, :]
-            xy, ex = cro[0, p, rows, :], cro[1, p, rows, :]
-            stiff = mod[0, p, rows, :] + 2.0 * mod[1, p, rows, :]
-            inv = 1.0 / den[p, rows, :]
-            den[p, rows, :] = inv
-            speed = jnp.sqrt(stiff * inv) * (
+            dens, lame, shear, xx, yy, xy, ex = (med[k, p, rows, :] for k in range(7))
+            inv = 1.0 / dens
+            med[0, p, rows, :] = inv
+            speed = jnp.sqrt((lame + 2.0 * shear) * inv) * (
                 jnp.sqrt(xx * xx + xy * xy) + jnp.sqrt(ex * ex + yy * yy)
             )
             return jnp.maximum(top, speed)
@@ -319,21 +309,31 @@
         )
         top = jnp.maximum(top, jnp.where(count[0] > p, part, 0.0))
     mine[...] = jnp.max(top, axis=0, keepdims=True)
-
-    def tell(d, _):
+    derive(fld)
+
+    def tell(i, _):
+        d = total - 1 - i
         pltpu.make_async_remote_copy(
             src_ref=mine,
             dst_ref=gather.at[d - 1],
-            send_sem=bsend.at[0],
-            recv_sem=brecv.at[0],
-            device_id=place(away(d)),
+            send_sem=send_sem.at[1],
+            recv_sem=recv_sem.at[1],
+            device_id=peer(d),
             device_id_type=MESH,
         ).start()
         return _
 
-    lax.fori_loop(1, total, tell, 0)
-
-    derive(fld)
+    lax.fori_loop(0, total - 1, tell, 0, unroll=unroll)
+    for j, off in enumerate(reach):
+        if j > 0:
+            pltpu.make_async_remote_copy(
+                src_ref=corner,
+                dst_ref=corners.at[reach.index(total - off)],
+                send_sem=send_sem.at[2],
+                recv_sem=recv_sem.at[2],
+                device_id=place(away(off)),
+                device_id_type=MESH,
+            ).start()
 
     def keep1(f, p, rows, value):
         rate1[f, p, rows, :] = value
@@ -341,15 +341,32 @@
     interior(keep1)
     collect(rate1, lines2)
     turn(lines2, turned2)
-    sent2 = post(turned2, outbox2, inbox2, send2, recv2)
-
-    for copy in sent1 + sentc:
-        copy.wait_recv()
+    post(turned2, outbox2, inbox2, 3)
+
+    box, local = [], []
+    for s in range(sides):
+        pos = jnp.int32(0)
+        for t in range(sides):
+            if t != s:
+                pos = pos + ((owner[t] == owner[s]) & (strip[t] < strip[s])).astype(jnp.int32)
+        pos = jnp.minimum(pos, slots - 1)
+        at = pos
+        for o, off in enumerate(offsets):
+            at = jnp.where(owner[s] == away(total - off), o * slots + pos, at)
+        box.append(at)
+        local.append(owner[s] == me)
+
+    settle(carried(inbox1), recv_sem.at[0])
     other = partners(turned1, inbox1)
     jump1 = [jnp.where(linked[s], weight * (other[s] - lines[s]), 0.0) for s in range(sides)]
     spread(jump1)
     add_rows(rate1, jump1)
     add_columns(rate1)
+
+    derive(rate1)
+
+    settle(gather, recv_sem.at[1])
+    settle(corners.at[pl.ds(1, len(reach) - 1)], recv_sem.at[2])
 
     def whole(value):
         return jnp.broadcast_to(value, (ROWS, n))
@@ -406,9 +423,6 @@
             theirs = jnp.where(edge, pltpu.roll(bend, n - (2 * s + 1), 1), 0.0)
             rest.append(theirs - mixed[side] - 2.0 * jump1[s] - lines2[s])
 
-    derive(rate1)
-
-    pltpu.make_async_copy(gather, gather, brecv.at[0]).wait()
     best = mine[...]
     for d in range(total - 1):
         best = jnp.maximum(best, gather[d])
@@ -422,8 +436,7 @@
 
     interior(keep2)
 
-    for copy in sent2:
-        copy.wait_recv()
+    settle(carried(inbox2), recv_sem.at[3])
     other = partners(turned2, inbox2)
     jump2 = [
         jnp.where(linked[s], (half * weight) * (other[s] + rest[s]), 0.0) for s in range(sides)
@@ -432,9 +445,10 @@
     add_rows(out_v, jump2)
     add_columns(out_v)
 
-    for copy in sent1 + sentc + sent2:
-        copy.wait_send()
-    pltpu.make_async_copy(gather, gather, bsend.at[0]).wait()
+    settle(carried(outbox1), send_sem.at[0])
+    settle(gather, send_sem.at[1])
+    settle(corners.at[pl.ds(1, len(reach) - 1)], send_sem.at[2])
+    settle(carried(outbox2), send_sem.at[3])
 
 
 def shards(
@@ -454,41 +468,35 @@
     state = pltpu.VMEM(fields.shape, f32)
     square = pltpu.VMEM((n, n), f32)
     dma = pltpu.SemaphoreType.DMA
-    boxed = pltpu.VMEM((4, slots, 8, n), f32)
-    arrived = pltpu.VMEM((4 * slots, 8, n), f32)
+    boxed = pltpu.VMEM((len(offsets) * slots, 8, n), f32)
     strips = pltpu.VMEM((slots * 4, 8, n), f32)
     return pl.pallas_call(
         functools.partial(kernel, total, subs, offsets, reach),
         out_shape=pltpu.VMEM(fields.shape, f32),
-        in_specs=[hbm] * 10,
+        in_specs=[hbm] * 9,
         out_specs=pl.BlockSpec(memory_space=pltpu.VMEM),
         scratch_shapes=[
             pltpu.SMEM(connectivity.shape[::-1], i32),
             pltpu.SMEM(count.shape, i32),
             pltpu.VMEM(extension.shape[::-1], f32),
-            square, square,
+            pltpu.VMEM((2, n, n), f32),
             state,
-            pltpu.VMEM(density.shape, f32),
-            pltpu.VMEM(moduli.shape, f32),
-            pltpu.VMEM(metric_diag.shape, f32),
-            pltpu.VMEM(metric_cross.shape, f32),
+            pltpu.VMEM((7,) + density.shape, f32),
             state, state, state,
             pltpu.VMEM((2 * n, 2 * n), jnp.bfloat16),
             pltpu.VMEM((2 * n, 2 * n), jnp.bfloat16),
             square, square, square,
             strips, strips, strips, strips,
-            boxed, boxed, arrived, arrived,
+            boxed, boxed, boxed, boxed,
             pltpu.VMEM((1, n), f32),
             pltpu.VMEM((len(reach), 1, n), f32),
             pltpu.VMEM((1, n), f32),
             pltpu.VMEM((total - 1, 1, n), f32),
-            dma((10,)),
-            dma((4,)), dma((4,)), dma((4,)), dma((4,)),
-            dma((len(reach) - 1,)), dma((len(reach) - 1,)), dma((1,)), dma((1,)),
+            dma((6,)), dma((4,)), dma((4,)),
         ],
         compiler_params=pltpu.CompilerParams(collective_id=0, has_side_effects=True),
     )(connectivity.T, count, fields, density, moduli, metric_diag, metric_cross, extension.T,
-      jnp.asarray(inner), jnp.asarray(outer))
+      jnp.asarray(np.stack([inner, outer])))
 
 
 def solution(mesh):

time: 13.9 us -> 13.3 us (0.957)
  Pallas kernels: 12.2 us -> 11.7 us
    pallas_call x1, Pallas kernels: 12.2 us -> 11.7 us  [shards(): pl.pallas_call(functools.partial(kernel, total, subs, offsets, reach), ou...]
where the time goes in v1:
time: 13.3 us; the launch traced here: 13.2 us
  Pallas kernels  11.7 us (88%)
  local copies, waits for them, and re-layouts  0.84 us (6%)
  between operations  0.66 us (5%)
    pallas_call x1, Pallas kernels, shards(): pl.pallas_call(functools.partial(kernel, total, subs, offsets, reach), ou...  11.7 us
    unnamed x1, local copies, waits for them, and re-layouts  0.84 us

profile of v1, /device:TPU:0, one launch (start us, length us, event | category | flops | bytes accessed | tf_op | source)
XLA Modules:
  0.0 13.2 jit_solution(13194711791860332586)
XLA Ops:
  0.7 11.7 %shard_map.91 = f32[5,2,128,128]{3,2,1,0:T(8,128)S(1)} custom-call(s32[3,8]{1,0:T(4,128)} %bitcast.3, s32[1]{0:T(128)S(6)} %copy.12.count_hbm, f32[5,2,128,128]{3,2,1,0:T(8,128)} %fields_hbm.1, f32[2,128,128]{2,1,0:T(8,128)} %density_hbm.1, f32[2,2,128,128]{3,2,1,0:T(8,128)} %moduli_hbm.1, f32[2,2,128,128]{3,2,1,0:T(8,128)} %diag_hbm.1, ...), custom_call_target="tpu_custom_call" | custom-call | tf_op jit(solution)/shard_map/pallas_call | solution.py:473
  12.3 0.8 %copy.11 = f32[5,2,128,128]{3,2,1,0:T(8,128)} copy(f32[5,2,128,128]{3,2,1,0:T(8,128)S(1)} %shard_map.91) | data formatting | bytes 1310720

commit v2 on v1

--- a/solution.py
+++ b/solution.py
@@ -25,9 +25,9 @@
     at = (np.arange(points)[:, None] - np.arange(length)[None, :]) % length
     full = kernel[at].astype(np.float32)
     padded = -(-extra // ROWS) * ROWS
-    outer = np.zeros((points, points), np.float32)
-    outer[:, :extra] = full[:, points:]
-    return full[:, :points], outer, padded
+    outer = np.zeros((padded, points), np.float32)
+    outer[:extra] = full[:, points:].T
+    return np.concatenate([full[:, :points].T, outer])
 
 
 def split(x):
@@ -43,7 +43,7 @@
     out_v,
     conn, count, ext, consts,
     fld, med, rate1, dxi, deta, left, right, ext_v, cols, trans,
-    lines, lines2, turned1, turned2, outbox1, outbox2, inbox1, inbox2, corner, corners,
+    lines, lines2, turned1, turned2, outbox1, outbox2, inbox1, inbox2,
     mine, gather,
     load_sem, send_sem, recv_sem,
 ):
@@ -77,22 +77,22 @@
         pltpu.make_async_copy(fields_hbm.at[f], fld.at[f], load_sem.at[4]).start()
     ext_load.start()
     consts_load.start()
+
+    barrier = pltpu.get_barrier_semaphore()
+
+    def greet(i, _):
+        pl.semaphore_signal(
+            barrier, inc=1, device_id=peer(total - 1 - i), device_id_type=MESH
+        )
+        return _
+
+    lax.fori_loop(0, total - 1, greet, 0, unroll=unroll)
     pltpu.make_async_copy(density_hbm, med.at[0], load_sem.at[5]).start()
     for k in range(2):
         pltpu.make_async_copy(moduli_hbm.at[k], med.at[1 + k], load_sem.at[5]).start()
         pltpu.make_async_copy(diag_hbm.at[k], med.at[3 + k], load_sem.at[5]).start()
         pltpu.make_async_copy(cross_hbm.at[k], med.at[5 + k], load_sem.at[5]).start()
     count_load.start()
-
-    barrier = pltpu.get_barrier_semaphore()
-
-    def greet(i, _):
-        pl.semaphore_signal(
-            barrier, inc=1, device_id=peer(total - 1 - i), device_id_type=MESH
-        )
-        return _
-
-    lax.fori_loop(0, total - 1, greet, 0, unroll=unroll)
 
     lines[...] = jnp.zeros_like(lines)
     lines2[...] = jnp.zeros_like(lines2)
@@ -126,6 +126,7 @@
     low, high = lane == 0, lane == n - 1
     edge = low | high
     used = row < comps
+    upper = lane >= n // 2
     pairs = [(f, p, p * 8 + f) for p in range(slots) for f in range(comps)]
     weight = penalty_weight * (n - 1)
 
@@ -153,12 +154,16 @@
             index = jnp.where(flip[s] == 1, n - 1 - lane, lane)
             turned[s] = jnp.take_along_axis(lines[s], index, axis=1)
 
-    def post(turned, outbox, inbox, at):
+    def post(turned, outbox, inbox, at, rider=None):
         for o in range(len(offsets)):
             for k in range(slots):
-                outbox[o * slots + k] = turned[picks[o][k]]
+                line = turned[picks[o][k]]
+                if rider is not None:
+                    line = jnp.where(row == comps, rider, line)
+                outbox[o * slots + k] = line
+        height = comps + (rider is not None)
         for o in range(len(offsets)):
-            spot = (pl.ds(o * slots, slots), pl.ds(0, comps), slice(None))
+            spot = (pl.ds(o * slots, slots), pl.ds(0, height), slice(None))
             pltpu.make_async_remote_copy(
                 src_ref=outbox.at[spot],
                 dst_ref=inbox.at[spot],
@@ -171,8 +176,11 @@
     def settle(buffer, sem):
         pltpu.make_async_copy(buffer, buffer, sem).wait()
 
-    def carried(buffer):
-        return buffer.at[:, pl.ds(0, comps), :]
+    def carried(buffer, height):
+        return buffer.at[:, pl.ds(0, height), :]
+
+    def whole(value):
+        return jnp.broadcast_to(value, (ROWS, n))
 
     def partners(turned, inbox):
         return [
@@ -243,34 +251,40 @@
 
         lax.fori_loop(0, chunks, body, 0, unroll=chunks)
 
+    fields_load.wait()
     ext_load.wait()
     consts_load.wait()
-    fields_load.wait()
     twice, extra = ext.shape
+    edges = twice // 2
     ext_v[pl.ds(0, twice), pl.ds(0, extra)] = ext[...]
-    turned = pltpu.roll(ext_v[...], n - twice // 2, 0)
-    matrix = consts[0] + lax.dot_general(
-        consts[1],
-        turned,
-        (((1,), (1,)), ((), ())),
+    bent = jnp.dot(
+        ext_v[...],
+        consts[pl.ds(n, ext_v.shape[1]), :],
         precision=lax.Precision.HIGHEST,
         preferred_element_type=jnp.float32,
     )
+    consts[pl.ds(n - edges, edges), :] = consts[pl.ds(n - edges, edges), :] + bent[:edges]
+    consts[pl.ds(0, edges), :] = consts[pl.ds(0, edges), :] + bent[edges:twice]
+    matrix = consts[pl.ds(0, n), :]
     hi, lo = split(matrix)
     none = jnp.zeros_like(hi)
+    right[...] = jnp.concatenate(
+        [jnp.concatenate([hi, lo], axis=1), jnp.concatenate([hi, none], axis=1)], axis=0
+    )
+    hi, lo = split(jnp.transpose(matrix))
     left[...] = jnp.concatenate(
         [jnp.concatenate([hi, hi], axis=1), jnp.concatenate([lo, none], axis=1)], axis=0
     )
-    hi, lo = split(jnp.transpose(matrix))
-    right[...] = jnp.concatenate(
-        [jnp.concatenate([hi, lo], axis=1), jnp.concatenate([hi, none], axis=1)], axis=0
-    )
-
     collect(fld, lines)
     turn(lines, turned1)
+    table = jnp.zeros((ROWS, n), jnp.int32)
+    for r in range(3):
+        for s in range(sides):
+            table = jnp.where(lane == r * sides + s, conn[r, s], table)
+    table = table.astype(jnp.float32)
 
     pl.semaphore_wait(barrier, total - 1)
-    post(turned1, outbox1, inbox1, 0)
+    post(turned1, outbox1, inbox1, 0, table)
 
     count_load.wait()
     med_load.wait()
@@ -280,16 +294,8 @@
             first = p * 4 + 2 * b
             rolled = pltpu.roll(lines[p * 4 + b], first + 1, 1)
             tile = jnp.where((lane == first) | (lane == first + 1), rolled, tile)
-    for r in range(3):
-        for s in range(sides):
-            tile = jnp.where(
-                (row == comps + r) & (lane == s), conn[r, s].astype(jnp.float32), tile
-            )
-    packed = jnp.sum(
-        pltpu.roll(tile, 0, 1, stride=sides, stride_axis=0), axis=0, keepdims=True
-    )
-    corner[...] = packed
-    corners[0] = packed
+    tile = pltpu.roll(jnp.where(used, tile, 0.0), 0, 1, stride=sides, stride_axis=0)
+    packed = jnp.sum(tile, axis=0, keepdims=True)
 
     top = jnp.zeros((ROWS, n), jnp.float32)
     for p in range(slots):
@@ -308,7 +314,8 @@
             0, chunks, speeds, jnp.zeros((ROWS, n), jnp.float32), unroll=chunks
         )
         top = jnp.maximum(top, jnp.where(count[0] > p, part, 0.0))
-    mine[...] = jnp.max(top, axis=0, keepdims=True)
+    top = jnp.max(jnp.maximum(top, pltpu.roll(top, n // 2, 1)), axis=0, keepdims=True)
+    mine[...] = jnp.where(upper[:1], top, packed)
     derive(fld)
 
     def tell(i, _):
@@ -324,16 +331,6 @@
         return _
 
     lax.fori_loop(0, total - 1, tell, 0, unroll=unroll)
-    for j, off in enumerate(reach):
-        if j > 0:
-            pltpu.make_async_remote_copy(
-                src_ref=corner,
-                dst_ref=corners.at[reach.index(total - off)],
-                send_sem=send_sem.at[2],
-                recv_sem=recv_sem.at[2],
-                device_id=place(away(off)),
-                device_id_type=MESH,
-            ).start()
 
     def keep1(f, p, rows, value):
         rate1[f, p, rows, :] = value
@@ -341,7 +338,7 @@
     interior(keep1)
     collect(rate1, lines2)
     turn(lines2, turned2)
-    post(turned2, outbox2, inbox2, 3)
+    post(turned2, outbox2, inbox2, 2)
 
     box, local = [], []
     for s in range(sides):
@@ -356,26 +353,19 @@
         box.append(at)
         local.append(owner[s] == me)
 
-    settle(carried(inbox1), recv_sem.at[0])
+    settle(carried(inbox1, comps + 1), recv_sem.at[0])
     other = partners(turned1, inbox1)
     jump1 = [jnp.where(linked[s], weight * (other[s] - lines[s]), 0.0) for s in range(sides)]
     spread(jump1)
     add_rows(rate1, jump1)
     add_columns(rate1)
-
     derive(rate1)
 
-    settle(gather, recv_sem.at[1])
-    settle(corners.at[pl.ds(1, len(reach) - 1)], recv_sem.at[2])
-
-    def whole(value):
-        return jnp.broadcast_to(value, (ROWS, n))
-
-    table = jnp.zeros((ROWS, n), jnp.float32)
-    for j in range(len(reach)):
-        index = (lane - j * sides + row * sides) & (n - 1)
-        laid = jnp.take_along_axis(whole(corners[j]), index, axis=1)
-        table = jnp.where((lane >= j * sides) & (lane < (j + 1) * sides), laid, table)
+    def keep2(f, p, rows, value):
+        out_v[f, p, rows, :] = value
+
+    interior(keep2)
+
     their_owner = jnp.full((ROWS, n), -1, jnp.int32)
     their_strip = jnp.zeros((ROWS, n), jnp.int32)
     their_flip = jnp.zeros((ROWS, n), jnp.int32)
@@ -385,10 +375,10 @@
         their_strip = jnp.where(here, strip[s], their_strip)
         their_flip = jnp.where(here, flip[s], their_flip)
 
-    def seat(device):
+    def seat(device, count):
         at = jnp.zeros((ROWS, n), jnp.int32)
-        for j, off in enumerate(reach):
-            at = jnp.where(device == away(off), j * sides, at)
+        for j in range(1, count):
+            at = jnp.where(device == away(reach[j]), j, at)
         return at
 
     def nook(strip, end):
@@ -396,18 +386,28 @@
         across = (strip & 2) == 0
         return (strip & ~3) + jnp.where(across, 2 * b + 1 - end, 2 * end + 1 - b)
 
+    def look(rows, seats, index):
+        found = jnp.zeros((ROWS, n), jnp.float32)
+        index = row * sides + index
+        for j, line in enumerate(rows):
+            found = jnp.where(seats == j, jnp.take_along_axis(line, index, axis=1), found)
+        return found
+
+    close = 1 + len(offsets)
+    tables = [table]
+    for j in range(1, close):
+        o = offsets.index(total - reach[j])
+        tables.append(whole(inbox1[o * slots, pl.ds(comps, 1), :]))
     end = (1 - (lane & 1)) ^ (their_flip & 1)
-    base = seat(their_owner)
+    base = seat(their_owner, close)
     beside = (their_strip & ~3) + jnp.where((their_strip & 2) == 0, 2 + end, end)
-    entry = jnp.take_along_axis(table, base + beside, axis=1)
-    own = jnp.take_along_axis(table, base + nook(their_strip, end), axis=1)
-    far_owner = whole(entry[comps : comps + 1]).astype(jnp.int32)
-    far_strip = whole(entry[comps + 1 : comps + 2]).astype(jnp.int32)
-    far_flip = whole(entry[comps + 2 : comps + 3]).astype(jnp.int32)
+    entry = look(tables, base, beside)
+    far_owner, far_strip, far_flip = (whole(entry[r : r + 1]).astype(jnp.int32) for r in range(3))
     far_strip = jnp.where(far_owner >= 0, far_strip, 0)
     far_end = (their_strip & 1) ^ (far_flip & 1)
-    value = jnp.take_along_axis(table, seat(far_owner) + nook(far_strip, far_end), axis=1)
-    bend = jnp.where((far_owner >= 0) & used, weight * (value - own), 0.0)
+    far_seat = seat(far_owner, len(reach))
+    far_nook = nook(far_strip, far_end)
+    near_nook = nook(their_strip, end)
 
     rest = []
     for p in range(slots):
@@ -420,23 +420,41 @@
         )
         for side in range(4):
             s = p * 4 + side
-            theirs = jnp.where(edge, pltpu.roll(bend, n - (2 * s + 1), 1), 0.0)
-            rest.append(theirs - mixed[side] - 2.0 * jump1[s] - lines2[s])
-
-    best = mine[...]
-    for d in range(total - 1):
-        best = jnp.maximum(best, gather[d])
-    bound = jnp.max(best, axis=1, keepdims=True)
+            rest.append(-mixed[side] - 2.0 * jump1[s] - lines2[s])
+
+    settle(gather, recv_sem.at[1])
+
+    def report(off):
+        if simple:
+            return gather[(me ^ away(off)) - 1]
+        return gather[total - off - 1]
+
+    reports = [whole(mine[...])] + [whole(report(off)) for off in reach[1:]]
+    value = look(reports, far_seat, far_nook)
+    own = look(reports[:close], base, near_nook)
+    bend = jnp.where((far_owner >= 0) & used, weight * (value - own), 0.0)
+    best = [mine[...]] + [gather[d] for d in range(total - 1)]
+    while len(best) > 1:
+        best = [jnp.maximum(*best[k : k + 2]) if k + 1 < len(best) else best[k]
+                for k in range(0, len(best), 2)]
+    bound = jnp.max(jnp.where(upper[:1], best[0], 0.0), axis=1, keepdims=True)
     step = jnp.broadcast_to(cfl_number / (bound * (n - 1)), (ROWS, n))
     half = 0.5 * step * step
-
-    def keep2(f, p, rows, second):
-        value = fld[f, p, rows, :] + step * rate1[f, p, rows, :] + half * second
-        out_v[f, p, rows, :] = jnp.where(count[0] > p, value, 0.0)
-
-    interior(keep2)
-
-    settle(carried(inbox2), recv_sem.at[3])
+    for p in range(slots):
+
+        def settled(c, _):
+            rows = pl.ds(pl.multiple_of(c * ROWS, ROWS), ROWS)
+            for f in range(comps):
+                value = fld[f, p, rows, :] + step * rate1[f, p, rows, :]
+                value = value + half * out_v[f, p, rows, :]
+                out_v[f, p, rows, :] = jnp.where(count[0] > p, value, 0.0)
+            return _
+
+        lax.fori_loop(0, chunks, settled, 0, unroll=chunks)
+    for s in range(sides):
+        rest[s] = rest[s] + jnp.where(edge, pltpu.roll(bend, n - (2 * s + 1), 1), 0.0)
+
+    settle(carried(inbox2, comps), recv_sem.at[2])
     other = partners(turned2, inbox2)
     jump2 = [
         jnp.where(linked[s], (half * weight) * (other[s] + rest[s]), 0.0) for s in range(sides)
@@ -445,17 +463,16 @@
     add_rows(out_v, jump2)
     add_columns(out_v)
 
-    settle(carried(outbox1), send_sem.at[0])
+    settle(carried(outbox1, comps + 1), send_sem.at[0])
     settle(gather, send_sem.at[1])
-    settle(corners.at[pl.ds(1, len(reach) - 1)], send_sem.at[2])
-    settle(carried(outbox2), send_sem.at[3])
+    settle(carried(outbox2, comps), send_sem.at[2])
 
 
 def shards(
     total, subs, fields, density, moduli, metric_diag, metric_cross, extension, count, connectivity
 ):
     comps, slots, n, _ = fields.shape
-    inner, outer, _ = circulant(n, extension.shape[0])
+    consts = circulant(n, extension.shape[0])
     far = total // 2 + 1
     offsets = (1, total - 1, far, total - far)
     reach = [0, *offsets]
@@ -479,24 +496,23 @@
             pltpu.SMEM(connectivity.shape[::-1], i32),
             pltpu.SMEM(count.shape, i32),
             pltpu.VMEM(extension.shape[::-1], f32),
-            pltpu.VMEM((2, n, n), f32),
+            pltpu.VMEM(consts.shape, f32),
             state,
             pltpu.VMEM((7,) + density.shape, f32),
             state, state, state,
             pltpu.VMEM((2 * n, 2 * n), jnp.bfloat16),
             pltpu.VMEM((2 * n, 2 * n), jnp.bfloat16),
-            square, square, square,
+            pltpu.VMEM((-(-extension.shape[1] // ROWS) * ROWS, consts.shape[0] - n), f32),
+            square, square,
             strips, strips, strips, strips,
             boxed, boxed, boxed, boxed,
             pltpu.VMEM((1, n), f32),
-            pltpu.VMEM((len(reach), 1, n), f32),
-            pltpu.VMEM((1, n), f32),
             pltpu.VMEM((total - 1, 1, n), f32),
-            dma((6,)), dma((4,)), dma((4,)),
+            dma((6,)), dma((3,)), dma((3,)),
         ],
         compiler_params=pltpu.CompilerParams(collective_id=0, has_side_effects=True),
     )(connectivity.T, count, fields, density, moduli, metric_diag, metric_cross, extension.T,
-      jnp.asarray(np.stack([inner, outer])))
+      jnp.asarray(consts))
 
 
 def solution(mesh):

time: 13.3 us -> 12.8 us (0.962)
  Pallas kernels: 11.7 us -> 11.2 us
    pallas_call x1, Pallas kernels: 11.7 us -> 11.2 us  [shards(): pl.pallas_call(functools.partial(kernel, total, subs, offsets, reach), ou...]
where the time goes in v2:
time: 12.8 us; the launch traced here: 12.7 us
  Pallas kernels  11.2 us (88%)
  local copies, waits for them, and re-layouts  0.84 us (7%)
  between operations  0.66 us (5%)
    pallas_call x1, Pallas kernels, shards(): pl.pallas_call(functools.partial(kernel, total, subs, offsets, reach), ou...  11.2 us
    unnamed x1, local copies, waits for them, and re-layouts  0.84 us

profile of v2, /device:TPU:0, one launch (start us, length us, event | category | flops | bytes accessed | tf_op | source)
XLA Modules:
  0.0 12.7 jit_solution(12577934448517395887)
XLA Ops:
  0.7 11.2 %shard_map.91 = f32[5,2,128,128]{3,2,1,0:T(8,128)S(1)} custom-call(s32[3,8]{1,0:T(4,128)} %bitcast.3, s32[1]{0:T(128)S(6)} %copy.12.count_hbm, f32[5,2,128,128]{3,2,1,0:T(8,128)} %fields_hbm.1, f32[2,128,128]{2,1,0:T(8,128)} %density_hbm.1, f32[2,2,128,128]{3,2,1,0:T(8,128)} %moduli_hbm.1, f32[2,2,128,128]{3,2,1,0:T(8,128)} %diag_hbm.1, ...), custom_call_target="tpu_custom_call" | custom-call | tf_op jit(solution)/shard_map/pallas_call | solution.py:490
  11.8 0.8 %copy.11 = f32[5,2,128,128]{3,2,1,0:T(8,128)} copy(f32[5,2,128,128]{3,2,1,0:T(8,128)S(1)} %shard_map.91) | data formatting | bytes 1310720

commit v3 on v2

--- a/solution.py
+++ b/solution.py
@@ -8,7 +8,7 @@
 from jax.experimental.pallas import tpu as pltpu
 from jax.sharding import PartitionSpec as P
 
-MESH = pl.DeviceIdType.MESH
+LOGICAL = pl.DeviceIdType.LOGICAL
 ROWS = 8
 cfl_number = 0.5
 penalty_weight = 0.5
@@ -40,9 +40,9 @@
     total, subs, offsets, reach,
     conn_hbm, count_hbm, fields_hbm, density_hbm, moduli_hbm, diag_hbm, cross_hbm,
     ext_hbm, consts_hbm,
-    out_v,
+    fld, rate1, rate2, cols, edges2, factors,
     conn, count, ext, consts,
-    fld, med, rate1, dxi, deta, left, right, ext_v, cols, trans,
+    med, dxi, deta, left, right, ext_v, trans,
     lines, lines2, turned1, turned2, outbox1, outbox2, inbox1, inbox2,
     mine, gather,
     load_sem, send_sem, recv_sem,
@@ -50,21 +50,15 @@
     comps, slots, n, _ = fld.shape
     sides = slots * 4
     chunks = n // ROWS
-    patch, core = lax.axis_index("patch"), lax.axis_index("sub")
-    me = patch * subs + core
-    simple = total & (total - 1) == 0 and subs & (subs - 1) == 0
+    me = lax.axis_index("patch") * subs + lax.axis_index("sub")
+    simple = total & (total - 1) == 0
     unroll = total - 1 if total <= 64 else 1
 
     def away(off):
         return lax.rem(me + off, total)
 
-    def place(flat):
-        return (lax.div(flat, subs), lax.rem(flat, subs))
-
     def peer(d):
-        if simple:
-            return (patch ^ lax.div(d, subs), core ^ lax.rem(d, subs))
-        return place(away(d))
+        return me ^ d if simple else away(d)
 
     conn_load = pltpu.make_async_copy(conn_hbm, conn, load_sem.at[0])
     count_load = pltpu.make_async_copy(count_hbm, count, load_sem.at[1])
@@ -73,27 +67,37 @@
     fields_load = pltpu.make_async_copy(fields_hbm, fld, load_sem.at[4])
     med_load = pltpu.make_async_copy(med, med, load_sem.at[5])
     conn_load.start()
+    ext_load.start()
+    tall = consts.shape[0] // 5
+    for k in range(5):
+        part = pl.ds(k * tall, tall)
+        pltpu.make_async_copy(consts_hbm.at[part], consts.at[part], load_sem.at[3]).start()
+
+    def fetch(src, dst, sem, cuts):
+        for p in range(slots):
+            for k in range(cuts):
+                part = (p, pl.ds(k * (n // cuts), n // cuts))
+                pltpu.make_async_copy(src.at[part], dst.at[part], sem).start()
+
     for f in range(comps):
-        pltpu.make_async_copy(fields_hbm.at[f], fld.at[f], load_sem.at[4]).start()
-    ext_load.start()
-    consts_load.start()
+        fetch(fields_hbm.at[f], fld.at[f], load_sem.at[4], 4)
+    count_load.start()
+    fetch(density_hbm, med.at[0], load_sem.at[5], 2)
+    for k in range(2):
+        fetch(moduli_hbm.at[k], med.at[1 + k], load_sem.at[5], 2)
+    for k in range(2):
+        fetch(diag_hbm.at[k], med.at[3 + k], load_sem.at[5], 2)
+        fetch(cross_hbm.at[k], med.at[5 + k], load_sem.at[5], 2)
 
     barrier = pltpu.get_barrier_semaphore()
 
     def greet(i, _):
         pl.semaphore_signal(
-            barrier, inc=1, device_id=peer(total - 1 - i), device_id_type=MESH
+            barrier, inc=1, device_id=peer(total - 1 - i), device_id_type=LOGICAL
         )
         return _
 
     lax.fori_loop(0, total - 1, greet, 0, unroll=unroll)
-    pltpu.make_async_copy(density_hbm, med.at[0], load_sem.at[5]).start()
-    for k in range(2):
-        pltpu.make_async_copy(moduli_hbm.at[k], med.at[1 + k], load_sem.at[5]).start()
-        pltpu.make_async_copy(diag_hbm.at[k], med.at[3 + k], load_sem.at[5]).start()
-        pltpu.make_async_copy(cross_hbm.at[k], med.at[5 + k], load_sem.at[5]).start()
-    count_load.start()
-
     lines[...] = jnp.zeros_like(lines)
     lines2[...] = jnp.zeros_like(lines2)
     trans[...] = jnp.zeros_like(trans)
@@ -126,7 +130,6 @@
     low, high = lane == 0, lane == n - 1
     edge = low | high
     used = row < comps
-    upper = lane >= n // 2
     pairs = [(f, p, p * 8 + f) for p in range(slots) for f in range(comps)]
     weight = penalty_weight * (n - 1)
 
@@ -169,8 +172,8 @@
                 dst_ref=inbox.at[spot],
                 send_sem=send_sem.at[at],
                 recv_sem=recv_sem.at[at],
-                device_id=place(near[o]),
-                device_id_type=MESH,
+                device_id=near[o],
+                device_id_type=LOGICAL,
             ).start()
 
     def settle(buffer, sem):
@@ -314,9 +317,7 @@
             0, chunks, speeds, jnp.zeros((ROWS, n), jnp.float32), unroll=chunks
         )
         top = jnp.maximum(top, jnp.where(count[0] > p, part, 0.0))
-    top = jnp.max(jnp.maximum(top, pltpu.roll(top, n // 2, 1)), axis=0, keepdims=True)
-    mine[...] = jnp.where(upper[:1], top, packed)
-    derive(fld)
+    mine[...] = jnp.concatenate([jnp.max(top, axis=0, keepdims=True), packed], axis=0)
 
     def tell(i, _):
         d = total - 1 - i
@@ -326,11 +327,13 @@
             send_sem=send_sem.at[1],
             recv_sem=recv_sem.at[1],
             device_id=peer(d),
-            device_id_type=MESH,
+            device_id_type=LOGICAL,
         ).start()
         return _
 
     lax.fori_loop(0, total - 1, tell, 0, unroll=unroll)
+
+    derive(fld)
 
     def keep1(f, p, rows, value):
         rate1[f, p, rows, :] = value
@@ -362,7 +365,7 @@
     derive(rate1)
 
     def keep2(f, p, rows, value):
-        out_v[f, p, rows, :] = value
+        rate2[f, p, rows, :] = value
 
     interior(keep2)
 
@@ -426,31 +429,24 @@
 
     def report(off):
         if simple:
-            return gather[(me ^ away(off)) - 1]
-        return gather[total - off - 1]
-
-    reports = [whole(mine[...])] + [whole(report(off)) for off in reach[1:]]
+            return gather[(me ^ away(off)) - 1, 1:]
+        return gather[total - off - 1, 1:]
+
+    reports = [whole(mine[1:])] + [whole(report(off)) for off in reach[1:]]
     value = look(reports, far_seat, far_nook)
     own = look(reports[:close], base, near_nook)
     bend = jnp.where((far_owner >= 0) & used, weight * (value - own), 0.0)
-    best = [mine[...]] + [gather[d] for d in range(total - 1)]
+    best = [mine[:1]] + [gather[d, :1] for d in range(total - 1)]
     while len(best) > 1:
         best = [jnp.maximum(*best[k : k + 2]) if k + 1 < len(best) else best[k]
                 for k in range(0, len(best), 2)]
-    bound = jnp.max(jnp.where(upper[:1], best[0], 0.0), axis=1, keepdims=True)
+    bound = jnp.max(best[0], axis=1, keepdims=True)
     step = jnp.broadcast_to(cfl_number / (bound * (n - 1)), (ROWS, n))
     half = 0.5 * step * step
+    factors[0] = step
+    factors[1] = half
     for p in range(slots):
-
-        def settled(c, _):
-            rows = pl.ds(pl.multiple_of(c * ROWS, ROWS), ROWS)
-            for f in range(comps):
-                value = fld[f, p, rows, :] + step * rate1[f, p, rows, :]
-                value = value + half * out_v[f, p, rows, :]
-                out_v[f, p, rows, :] = jnp.where(count[0] > p, value, 0.0)
-            return _
-
-        lax.fori_loop(0, chunks, settled, 0, unroll=chunks)
+        factors[2 + p] = jnp.where(count[0] > p, 1.0, 0.0) + jnp.zeros((ROWS, n), jnp.float32)
     for s in range(sides):
         rest[s] = rest[s] + jnp.where(edge, pltpu.roll(bend, n - (2 * s + 1), 1), 0.0)
 
@@ -460,12 +456,36 @@
         jnp.where(linked[s], (half * weight) * (other[s] + rest[s]), 0.0) for s in range(sides)
     ]
     spread(jump2)
-    add_rows(out_v, jump2)
-    add_columns(out_v)
+    for s in range(sides):
+        edges2[s] = jump2[s]
 
     settle(carried(outbox1, comps + 1), send_sem.at[0])
     settle(gather, send_sem.at[1])
     settle(carried(outbox2, comps), send_sem.at[2])
+
+
+def finish(fld, rate1, rate2, cols, edges2, factors, out_hbm, out_v, sem):
+    comps, slots, n, _ = fld.shape
+    chunks = n // ROWS
+    lane = lax.broadcasted_iota(jnp.int32, (ROWS, n), 1)
+    row = lax.broadcasted_iota(jnp.int32, (ROWS, n), 0)
+    edge = (lane == 0) | (lane == n - 1)
+    step, half = factors[0], factors[1]
+    for p in range(slots):
+        live = factors[2 + p] > 0.0
+        for f in range(comps):
+            for c in range(chunks):
+                rows = pl.ds(c * ROWS, ROWS)
+                side = pltpu.roll(cols[rows, :], n - (2 * (p * 8 + f) + 1), 1)
+                value = fld[f, p, rows, :] + step * rate1[f, p, rows, :]
+                value = value + half * rate2[f, p, rows, :] + jnp.where(edge, side, 0.0)
+                for side, at in ((0, 0), (1, chunks - 1)):
+                    if c == at:
+                        line = jnp.broadcast_to(edges2[p * 4 + side, pl.ds(f, 1), :], (ROWS, n))
+                        value = value + jnp.where(row == side * (ROWS - 1), line, 0.0)
+                out_v[f, p, rows, :] = jnp.where(live, value, 0.0)
+            pltpu.make_async_copy(out_v.at[f, p], out_hbm.at[f, p], sem.at[0]).start()
+    pltpu.make_async_copy(out_v, out_hbm, sem.at[0]).wait()
 
 
 def shards(
@@ -487,32 +507,41 @@
     dma = pltpu.SemaphoreType.DMA
     boxed = pltpu.VMEM((len(offsets) * slots, 8, n), f32)
     strips = pltpu.VMEM((slots * 4, 8, n), f32)
-    return pl.pallas_call(
+    factors = pltpu.VMEM((2 + slots, ROWS, n), f32)
+    vmem = pl.BlockSpec(memory_space=pltpu.VMEM)
+    parts = pl.pallas_call(
         functools.partial(kernel, total, subs, offsets, reach),
-        out_shape=pltpu.VMEM(fields.shape, f32),
+        out_shape=[state, state, state, square, strips, factors],
         in_specs=[hbm] * 9,
-        out_specs=pl.BlockSpec(memory_space=pltpu.VMEM),
+        out_specs=[vmem] * 6,
         scratch_shapes=[
             pltpu.SMEM(connectivity.shape[::-1], i32),
             pltpu.SMEM(count.shape, i32),
             pltpu.VMEM(extension.shape[::-1], f32),
             pltpu.VMEM(consts.shape, f32),
-            state,
             pltpu.VMEM((7,) + density.shape, f32),
-            state, state, state,
+            state, state,
             pltpu.VMEM((2 * n, 2 * n), jnp.bfloat16),
             pltpu.VMEM((2 * n, 2 * n), jnp.bfloat16),
             pltpu.VMEM((-(-extension.shape[1] // ROWS) * ROWS, consts.shape[0] - n), f32),
-            square, square,
+            square,
             strips, strips, strips, strips,
             boxed, boxed, boxed, boxed,
-            pltpu.VMEM((1, n), f32),
-            pltpu.VMEM((total - 1, 1, n), f32),
+            pltpu.VMEM((2, n), f32),
+            pltpu.VMEM((total - 1, 2, n), f32),
             dma((6,)), dma((3,)), dma((3,)),
         ],
         compiler_params=pltpu.CompilerParams(collective_id=0, has_side_effects=True),
     )(connectivity.T, count, fields, density, moduli, metric_diag, metric_cross, extension.T,
       jnp.asarray(consts))
+    return pl.pallas_call(
+        finish,
+        out_shape=jax.ShapeDtypeStruct(fields.shape, f32),
+        in_specs=[vmem] * 6,
+        out_specs=hbm,
+        scratch_shapes=[state, dma((1,))],
+        compiler_params=pltpu.CompilerParams(vmem_limit_bytes=8 * 2**20),
+    )(*parts)
 
 
 def solution(mesh):

time: 12.8 us -> 12.4 us (0.969)
  local copies, waits for them, and re-layouts: 0.84 us -> 0 us
  Pallas kernels: 11.2 us -> 11.5 us
    pallas_call x0 -> x1, Pallas kernels: none -> 0.92 us  [shards(): pl.pallas_call(finish, out_shape=jax.ShapeDtypeStruct(fields.shape, f32),...]
    unnamed x1 -> x0, local copies, waits for them, and re-layouts: 0.84 us -> none
    pallas_call x1, Pallas kernels: 11.2 us -> 10.6 us  [shards(): pl.pallas_call(functools.partial(kernel, total, subs, offsets, reach), ou...]
where the time goes in v3:
time: 12.4 us; the launch traced here: 12.2 us
  Pallas kernels  11.5 us (93%)
  between operations  0.66 us (5%)
    pallas_call x1, Pallas kernels, shards(): pl.pallas_call(functools.partial(kernel, total, subs, offsets, reach), ou...  10.6 us
    pallas_call x1, Pallas kernels, shards(): pl.pallas_call(finish, out_shape=jax.ShapeDtypeStruct(fields.shape, f32),...  0.92 us

profile of v3, /device:TPU:0, one launch (start us, length us, event | category | flops | bytes accessed | tf_op | source)
XLA Modules:
  0.0 12.2 jit_solution(284266080916614957)
XLA Ops:
  0.7 10.6 %shard_map.91 = (f32[5,2,128,128]{3,2,1,0:T(8,128)S(1)}, f32[5,2,128,128]{3,2,1,0:T(8,128)S(1)}, f32[5,2,128,128]{3,2,1,0:T(8,128)S(1)}, f32[128,128]{1,0:T(8,12...) custom-call(s32[3,8]{1,0:T(4,128)} %bitcast.3, s32[1]{0:T(128)S(6)} %copy.10.count_hbm, ...), custom_call_target="tpu_custom_call" | custom-call | tf_op jit(solution)/shard_map/pallas_call | solution.py:512
  11.3 0.9 %shard_map.92 = f32[5,2,128,128]{3,2,1,0:T(8,128)} custom-call(f32[5,2,128,128]{3,2,1,0:T(8,128)S(1)} %get-tuple-element.11.fld, f32[5,2,128,128]{3,2,1,0:T(8,128)S(1)} %get-tuple-element.12.rate1, f32[5,2,128,128]{3,2,1,0:T(8,128)S(1)} %get-tuple-element.13.rate2, f32[128,128]{1,0:T(8,128)S(1)} %get-tuple-element.14.cols, ...), custom_call_target="tpu_custom_call" | custom-call | tf_op jit(solution)/shard_map/pallas_call | solution.py:537

commit v4 on v3

--- a/solution.py
+++ b/solution.py
@@ -42,9 +42,9 @@
     ext_hbm, consts_hbm,
     fld, rate1, rate2, cols, edges2, factors,
     conn, count, ext, consts,
-    med, dxi, deta, left, right, ext_v, trans,
+    med, dxi, deta, left, right, ext_v, trans, thin, wide, tall, along, rims,
     lines, lines2, turned1, turned2, outbox1, outbox2, inbox1, inbox2,
-    mine, gather,
+    mine, gather, tally,
     load_sem, send_sem, recv_sem,
 ):
     comps, slots, n, _ = fld.shape
@@ -68,9 +68,9 @@
     med_load = pltpu.make_async_copy(med, med, load_sem.at[5])
     conn_load.start()
     ext_load.start()
-    tall = consts.shape[0] // 5
+    share = consts.shape[0] // 5
     for k in range(5):
-        part = pl.ds(k * tall, tall)
+        part = pl.ds(k * share, share)
         pltpu.make_async_copy(consts_hbm.at[part], consts.at[part], load_sem.at[3]).start()
 
     def fetch(src, dst, sem, cuts):
@@ -81,6 +81,15 @@
 
     for f in range(comps):
         fetch(fields_hbm.at[f], fld.at[f], load_sem.at[4], 4)
+    barrier = pltpu.get_barrier_semaphore()
+
+    def greet(i, _):
+        pl.semaphore_signal(
+            barrier, inc=1, device_id=peer(1 + i), device_id_type=LOGICAL
+        )
+        return _
+
+    lax.fori_loop(0, total - 1, greet, 0, unroll=unroll)
     count_load.start()
     fetch(density_hbm, med.at[0], load_sem.at[5], 2)
     for k in range(2):
@@ -89,15 +98,6 @@
         fetch(diag_hbm.at[k], med.at[3 + k], load_sem.at[5], 2)
         fetch(cross_hbm.at[k], med.at[5 + k], load_sem.at[5], 2)
 
-    barrier = pltpu.get_barrier_semaphore()
-
-    def greet(i, _):
-        pl.semaphore_signal(
-            barrier, inc=1, device_id=peer(total - 1 - i), device_id_type=LOGICAL
-        )
-        return _
-
-    lax.fori_loop(0, total - 1, greet, 0, unroll=unroll)
     lines[...] = jnp.zeros_like(lines)
     lines2[...] = jnp.zeros_like(lines2)
     trans[...] = jnp.zeros_like(trans)
@@ -130,10 +130,12 @@
     low, high = lane == 0, lane == n - 1
     edge = low | high
     used = row < comps
-    pairs = [(f, p, p * 8 + f) for p in range(slots) for f in range(comps)]
     weight = penalty_weight * (n - 1)
 
     def collect(state, lines):
+        kinds = state.shape[0]
+        pairs = [(f, p, p * 8 + f) for p in range(slots) for f in range(kinds)]
+
         def columns(c, _):
             rows = pl.ds(pl.multiple_of(c * ROWS, ROWS), ROWS)
             acc = jnp.zeros((ROWS, n), jnp.float32)
@@ -148,7 +150,7 @@
         for p in range(slots):
             lines[p * 4 + 2] = trans[pl.ds(p * 16 + 1, 8, stride=2), :]
             lines[p * 4 + 3] = trans[pl.ds(p * 16, 8, stride=2), :]
-            for f in range(comps):
+            for f in range(kinds):
                 lines[p * 4, pl.ds(f, 1)] = state[f, p, pl.ds(0, 1), :]
                 lines[p * 4 + 1, pl.ds(f, 1)] = state[f, p, pl.ds(n - 1, 1), :]
 
@@ -170,7 +172,7 @@
             pltpu.make_async_remote_copy(
                 src_ref=outbox.at[spot],
                 dst_ref=inbox.at[spot],
-                send_sem=send_sem.at[at],
+                send_sem=send_sem.at[0],
                 recv_sem=recv_sem.at[at],
                 device_id=near[o],
                 device_id_type=LOGICAL,
@@ -235,24 +237,6 @@
                 return _
 
             lax.fori_loop(0, chunks, body, 0, unroll=chunks)
-
-    def add_rows(state, jump):
-        for p in range(slots):
-            for f in range(comps):
-                for side, at in ((0, 0), (1, n - 1)):
-                    spot = pl.ds(at, 1)
-                    state[f, p, spot, :] = state[f, p, spot, :] + jump[p * 4 + side][f : f + 1]
-
-    def add_columns(state):
-        def body(c, _):
-            rows = pl.ds(pl.multiple_of(c * ROWS, ROWS), ROWS)
-            both = cols[rows, :]
-            for f, p, m in pairs:
-                side = pltpu.roll(both, n - (2 * m + 1), 1)
-                state[f, p, rows, :] = state[f, p, rows, :] + jnp.where(edge, side, 0.0)
-            return _
-
-        lax.fori_loop(0, chunks, body, 0, unroll=chunks)
 
     fields_load.wait()
     ext_load.wait()
@@ -292,12 +276,12 @@
     count_load.wait()
     med_load.wait()
     tile = jnp.zeros((ROWS, n), jnp.float32)
+    place = lane - row * sides
     for p in range(slots):
         for b in range(2):
             first = p * 4 + 2 * b
-            rolled = pltpu.roll(lines[p * 4 + b], first + 1, 1)
-            tile = jnp.where((lane == first) | (lane == first + 1), rolled, tile)
-    tile = pltpu.roll(jnp.where(used, tile, 0.0), 0, 1, stride=sides, stride_axis=0)
+            laid = pltpu.roll(lines[p * 4 + b], first + 1, 1, stride=sides, stride_axis=0)
+            tile = jnp.where(used & ((place == first) | (place == first + 1)), laid, tile)
     packed = jnp.sum(tile, axis=0, keepdims=True)
 
     top = jnp.zeros((ROWS, n), jnp.float32)
@@ -308,10 +292,10 @@
             dens, lame, shear, xx, yy, xy, ex = (med[k, p, rows, :] for k in range(7))
             inv = 1.0 / dens
             med[0, p, rows, :] = inv
-            speed = jnp.sqrt((lame + 2.0 * shear) * inv) * (
-                jnp.sqrt(xx * xx + xy * xy) + jnp.sqrt(ex * ex + yy * yy)
-            )
-            return jnp.maximum(top, speed)
+            along_x, along_y = xx * xx + xy * xy, ex * ex + yy * yy
+            both = along_x * along_y
+            square = along_x + along_y + 2.0 * (both * lax.rsqrt(both))
+            return jnp.maximum(top, (lame + 2.0 * shear) * inv * square)
 
         part = lax.fori_loop(
             0, chunks, speeds, jnp.zeros((ROWS, n), jnp.float32), unroll=chunks
@@ -324,7 +308,7 @@
         pltpu.make_async_remote_copy(
             src_ref=mine,
             dst_ref=gather.at[d - 1],
-            send_sem=send_sem.at[1],
+            send_sem=send_sem.at[0],
             recv_sem=recv_sem.at[1],
             device_id=peer(d),
             device_id_type=LOGICAL,
@@ -356,18 +340,100 @@
         box.append(at)
         local.append(owner[s] == me)
 
+    def keep2(f, p, rows, value):
+        rate2[f, p, rows, :] = value
+
+    derive(rate1)
+    interior(keep2)
+    collect(med, rims)
+    block = lax.broadcasted_iota(jnp.int32, (n, n), 1)
+    matrix = jnp.transpose(consts[pl.ds(0, n), :])
+    hi = matrix.astype(jnp.bfloat16).astype(jnp.float32)
+    thin[...] = jnp.where(
+        block < 2,
+        pltpu.roll(hi, 1, 1),
+        jnp.where(
+            block < 4,
+            pltpu.roll(hi, 3, 1),
+            jnp.where(block < 6, pltpu.roll(matrix - hi, 5, 1), 0.0),
+        ),
+    ).astype(jnp.bfloat16)
+    tall[...] = jnp.zeros_like(tall)
+    wide[...] = jnp.zeros_like(wide)
+    first, last = consts[pl.ds(0, 1), :], consts[pl.ds(n - 1, 1), :]
+    deep = lax.broadcasted_iota(jnp.int32, (2 * ROWS, n), 0)
+
+    def pieces(value):
+        hi = value.astype(jnp.bfloat16).astype(jnp.float32)
+        return hi, value - hi
+
+    first_hi, first_lo = pieces(first)
+    last_hi, last_lo = pieces(last)
+    for k, (one, two) in enumerate(
+        ((first_hi, last_hi), (first_hi, last_hi), (first_lo, last_lo))
+    ):
+        one = jnp.broadcast_to(one, (2 * ROWS, n))
+        two = jnp.broadcast_to(two, (2 * ROWS, n))
+        for f in range(comps):
+            slab = jnp.where(deep == 2 * f + 1, one, jnp.where(deep == 2 * f, two, 0.0))
+            slab = slab.astype(jnp.bfloat16)
+            for p in range(slots):
+                wide[pl.ds((k * slots + p) * 16, 16), pl.ds((f * slots + p) * n, n)] = slab
+
     settle(carried(inbox1, comps + 1), recv_sem.at[0])
     other = partners(turned1, inbox1)
     jump1 = [jnp.where(linked[s], weight * (other[s] - lines[s]), 0.0) for s in range(sides)]
-    spread(jump1)
-    add_rows(rate1, jump1)
-    add_columns(rate1)
-    derive(rate1)
-
-    def keep2(f, p, rows, value):
-        rate2[f, p, rows, :] = value
-
-    interior(keep2)
+    for p in range(slots):
+        parts = [pieces(jump1[p * 4 + side]) for side in range(4)]
+        for k, at in enumerate((0, 1, 0)):
+            low_rows = (k * slots + p) * 16
+            trans[pl.ds(low_rows + 1, 8, stride=2), :] = parts[2][at]
+            trans[pl.ds(low_rows, 8, stride=2), :] = parts[3][at]
+        (west_hi, west_lo), (east_hi, east_lo) = parts[0], parts[1]
+        for f in range(comps):
+            near_hi, near_lo = whole(west_hi[f : f + 1]), whole(west_lo[f : f + 1])
+            far_hi, far_lo = whole(east_hi[f : f + 1]), whole(east_lo[f : f + 1])
+            slab = jnp.where((row == 1) | (row == 5), near_hi, 0.0)
+            slab = jnp.where((row == 0) | (row == 4), far_hi, slab)
+            slab = jnp.where(row == 2, far_lo, jnp.where(row == 3, near_lo, slab))
+            slab = jnp.concatenate([slab, jnp.zeros_like(slab)], axis=0)
+            tall[pl.ds(0, 16), pl.ds((f * slots + p) * n, n)] = slab.astype(jnp.bfloat16)
+    stacked = jnp.concatenate(jump1, axis=0)
+    hi, lo = split(stacked)
+    slope = jnp.dot(
+        jnp.concatenate([hi, lo], axis=1), right[...], preferred_element_type=jnp.float32
+    )
+    slope = slope[:, :n] + slope[:, n:]
+    for s in range(sides):
+        along[s] = slope[s * ROWS : (s + 1) * ROWS]
+    for f in range(comps):
+        span = pl.ds(f * slots * n, slots * n)
+        xi = jnp.dot(thin[...], tall[:, span], preferred_element_type=jnp.float32)
+        for p in range(slots):
+            dxi[f, p] = xi[:, p * n : (p + 1) * n]
+    upright = jnp.transpose(trans[...]).astype(jnp.bfloat16)
+    for f in range(comps):
+        span = pl.ds(f * slots * n, slots * n)
+        eta = jnp.dot(upright, wide[:, span], preferred_element_type=jnp.float32)
+        for p in range(slots):
+            deta[f, p] = eta[:, p * n : (p + 1) * n]
+
+    def keep3(f, p, rows, value):
+        rate2[f, p, rows, :] = rate2[f, p, rows, :] + value
+
+    interior(keep3)
+    for s in range(sides):
+        inv, lame, shear, xx, yy, xy, ex = (rims[s, pl.ds(k, 1), :] for k in range(7))
+        stiff = lame + 2.0 * shear
+        lean = [along[s, pl.ds(f, 1), :] for f in range(comps)]
+        to_x, to_y = (ex, yy) if s % 4 < 2 else (xx, xy)
+        gx = [to_x * a for a in lean]
+        gy = [to_y * a for a in lean]
+        along[s, pl.ds(0, 1), :] = (gx[2] + gy[4]) * inv
+        along[s, pl.ds(1, 1), :] = (gx[4] + gy[3]) * inv
+        along[s, pl.ds(2, 1), :] = stiff * gx[0] + lame * gy[1]
+        along[s, pl.ds(3, 1), :] = lame * gx[0] + stiff * gy[1]
+        along[s, pl.ds(4, 1), :] = shear * (gy[0] + gx[1])
 
     their_owner = jnp.full((ROWS, n), -1, jnp.int32)
     their_strip = jnp.zeros((ROWS, n), jnp.int32)
@@ -440,28 +506,28 @@
     while len(best) > 1:
         best = [jnp.maximum(*best[k : k + 2]) if k + 1 < len(best) else best[k]
                 for k in range(0, len(best), 2)]
-    bound = jnp.max(best[0], axis=1, keepdims=True)
+    bound = jnp.sqrt(jnp.max(best[0], axis=1, keepdims=True))
     step = jnp.broadcast_to(cfl_number / (bound * (n - 1)), (ROWS, n))
     half = 0.5 * step * step
     factors[0] = step
     factors[1] = half
     for p in range(slots):
         factors[2 + p] = jnp.where(count[0] > p, 1.0, 0.0) + jnp.zeros((ROWS, n), jnp.float32)
+    early = [step * jump1[s] + half * along[s] for s in range(sides)]
     for s in range(sides):
         rest[s] = rest[s] + jnp.where(edge, pltpu.roll(bend, n - (2 * s + 1), 1), 0.0)
 
     settle(carried(inbox2, comps), recv_sem.at[2])
     other = partners(turned2, inbox2)
     jump2 = [
-        jnp.where(linked[s], (half * weight) * (other[s] + rest[s]), 0.0) for s in range(sides)
+        early[s] + jnp.where(linked[s], (half * weight) * (other[s] + rest[s]), 0.0)
+        for s in range(sides)
     ]
     spread(jump2)
     for s in range(sides):
         edges2[s] = jump2[s]
 
-    settle(carried(outbox1, comps + 1), send_sem.at[0])
-    settle(gather, send_sem.at[1])
-    settle(carried(outbox2, comps), send_sem.at[2])
+    settle(tally, send_sem.at[0])
 
 
 def finish(fld, rate1, rate2, cols, edges2, factors, out_hbm, out_v, sem):
@@ -484,7 +550,9 @@
                         line = jnp.broadcast_to(edges2[p * 4 + side, pl.ds(f, 1), :], (ROWS, n))
                         value = value + jnp.where(row == side * (ROWS - 1), line, 0.0)
                 out_v[f, p, rows, :] = jnp.where(live, value, 0.0)
-            pltpu.make_async_copy(out_v.at[f, p], out_hbm.at[f, p], sem.at[0]).start()
+                if (c + 1) % 4 == 0:
+                    part = (f, p, pl.ds((c - 3) * ROWS, 4 * ROWS))
+                    pltpu.make_async_copy(out_v.at[part], out_hbm.at[part], sem.at[0]).start()
     pltpu.make_async_copy(out_v, out_hbm, sem.at[0]).wait()
 
 
@@ -525,11 +593,16 @@
             pltpu.VMEM((2 * n, 2 * n), jnp.bfloat16),
             pltpu.VMEM((-(-extension.shape[1] // ROWS) * ROWS, consts.shape[0] - n), f32),
             square,
+            pltpu.VMEM((n, n), jnp.bfloat16),
+            pltpu.VMEM((n, comps * slots * n), jnp.bfloat16),
+            pltpu.VMEM((n, comps * slots * n), jnp.bfloat16),
+            strips, strips,
             strips, strips, strips, strips,
             boxed, boxed, boxed, boxed,
             pltpu.VMEM((2, n), f32),
             pltpu.VMEM((total - 1, 2, n), f32),
-            dma((6,)), dma((3,)), dma((3,)),
+            pltpu.VMEM((total - 1 + len(offsets) * slots * (2 * comps + 1) // 2, 2, n), f32),
+            dma((6,)), dma((1,)), dma((3,)),
         ],
         compiler_params=pltpu.CompilerParams(collective_id=0, has_side_effects=True),
     )(connectivity.T, count, fields, density, moduli, metric_diag, metric_cross, extension.T,

time: 12.4 us -> 12.3 us (level)
  no operation moved by 1% of the time
where the time goes in v4:
time: 12.3 us; the launch traced here: 12.1 us
  Pallas kernels  11.4 us (93%)
  between operations  0.66 us (5%)
    pallas_call x1, Pallas kernels, shards(): pl.pallas_call(functools.partial(kernel, total, subs, offsets, reach), ou...  10.5 us
    pallas_call x1, Pallas kernels, shards(): pl.pallas_call(finish, out_shape=jax.ShapeDtypeStruct(fields.shape, f32),...  0.89 us

profile of v4, /device:TPU:0, one launch (start us, length us, event | category | flops | bytes accessed | tf_op | source)
XLA Modules:
  0.0 12.1 jit_solution(574390152302386358)
XLA Ops:
  0.7 10.5 %shard_map.91 = (f32[5,2,128,128]{3,2,1,0:T(8,128)S(1)}, f32[5,2,128,128]{3,2,1,0:T(8,128)S(1)}, f32[5,2,128,128]{3,2,1,0:T(8,128)S(1)}, f32[128,128]{1,0:T(8,12...) custom-call(s32[3,8]{1,0:T(4,128)} %bitcast.3, s32[1]{0:T(128)S(6)} %copy.10.count_hbm, ...), custom_call_target="tpu_custom_call" | custom-call | tf_op jit(solution)/shard_map/pallas_call | solution.py:580
  11.2 0.9 %shard_map.92 = f32[5,2,128,128]{3,2,1,0:T(8,128)} custom-call(f32[5,2,128,128]{3,2,1,0:T(8,128)S(1)} %get-tuple-element.11.fld, f32[5,2,128,128]{3,2,1,0:T(8,128)S(1)} %get-tuple-element.12.rate1, f32[5,2,128,128]{3,2,1,0:T(8,128)S(1)} %get-tuple-element.13.rate2, f32[128,128]{1,0:T(8,128)S(1)} %get-tuple-element.14.cols, ...), custom_call_target="tpu_custom_call" | custom-call | tf_op jit(solution)/shard_map/pallas_call | solution.py:610

commit v5 on v4

--- a/solution.py
+++ b/solution.py
@@ -506,8 +506,8 @@
     while len(best) > 1:
         best = [jnp.maximum(*best[k : k + 2]) if k + 1 < len(best) else best[k]
                 for k in range(0, len(best), 2)]
-    bound = jnp.sqrt(jnp.max(best[0], axis=1, keepdims=True))
-    step = jnp.broadcast_to(cfl_number / (bound * (n - 1)), (ROWS, n))
+    square = jnp.broadcast_to(jnp.max(best[0], axis=1, keepdims=True), (ROWS, n))
+    step = (cfl_number / (n - 1)) * lax.rsqrt(square)
     half = 0.5 * step * step
     factors[0] = step
     factors[1] = half

time: 12.3 us -> 12.3 us (level)
  no operation moved by 1% of the time
where the time goes in v5:
time: 12.3 us; the launch traced here: 12.1 us
  Pallas kernels  11.4 us (93%)
  between operations  0.66 us (5%)
    pallas_call x1, Pallas kernels, shards(): pl.pallas_call(functools.partial(kernel, total, subs, offsets, reach), ou...  10.5 us
    pallas_call x1, Pallas kernels, shards(): pl.pallas_call(finish, out_shape=jax.ShapeDtypeStruct(fields.shape, f32),...  0.89 us

profile of v5, /device:TPU:0, one launch (start us, length us, event | category | flops | bytes accessed | tf_op | source)
XLA Modules:
  0.0 12.1 jit_solution(16050858437707976653)
XLA Ops:
  0.7 10.5 %shard_map.91 = (f32[5,2,128,128]{3,2,1,0:T(8,128)S(1)}, f32[5,2,128,128]{3,2,1,0:T(8,128)S(1)}, f32[5,2,128,128]{3,2,1,0:T(8,128)S(1)}, f32[128,128]{1,0:T(8,12...) custom-call(s32[3,8]{1,0:T(4,128)} %bitcast.3, s32[1]{0:T(128)S(6)} %copy.10.count_hbm, ...), custom_call_target="tpu_custom_call" | custom-call | tf_op jit(solution)/shard_map/pallas_call | solution.py:580
  11.2 0.9 %shard_map.92 = f32[5,2,128,128]{3,2,1,0:T(8,128)} custom-call(f32[5,2,128,128]{3,2,1,0:T(8,128)S(1)} %get-tuple-element.11.fld, f32[5,2,128,128]{3,2,1,0:T(8,128)S(1)} %get-tuple-element.12.rate1, f32[5,2,128,128]{3,2,1,0:T(8,128)S(1)} %get-tuple-element.13.rate2, f32[128,128]{1,0:T(8,128)S(1)} %get-tuple-element.14.cols, ...), custom_call_target="tpu_custom_call" | custom-call | tf_op jit(solution)/shard_map/pallas_call | solution.py:610
